TPU v7x, 32 devices: a whole 2x2x4 slice. The times are simulated.
32 devices in a mesh: row: 8 (over z, core), col: 4 (over y, x).
Axes of the slice: x: 2, y: 2, z: 4, core: 2. Of those that a mesh axis runs over, the one named last changes fastest.
Arguments:
- blocks: bfloat16 [128, 8, 256, 256], P('row', 'col'), may hold values from -0.125 to 0.125
- block_cols: int32 [128, 8], P('row', 'col'), may hold values from 0 to 48, as said below
- objective: float32 [49152], P(('col', 'row')), may hold values from -6 to 6
- lower_bound: float32 [49152], P(('col', 'row')), may hold values from -1 to -0.2
- upper_bound: float32 [49152], P(('col', 'row')), may hold values from 0.2 to 1
- right_side: float32 [32768], P(('row', 'col')), may hold values from -6 to 6
- primal_init: float32 [49152], P(('col', 'row')), may hold values from -0.2 to 0.2
- dual_init: float32 [32768], P(('row', 'col')), may hold values from 0 to 1
Outputs:
- primal_final: float32 [49152], P(('col', 'row'))
- dual_final: float32 [32768], P(('row', 'col'))
- step_norms: float32 [8, 2], replicated
Inputs may be any that keep to these rules, and one draw needn't show every extreme that they name: `block_cols`: entry j of a row block indexes column group j // 2; its live entries (below 48) are distinct within one row block and group, 48 marks an empty slot, and in every draw some row block has all 2 slots of some group live.
All inputs are finite; a program needn't handle non-finite values.
Results may differ from a plain program's by a relative error of at most 0.0015.
Values may be sent and summed in bfloat16 or wider, within the bound.
No kernel may reach another device: no remote copies, remote signals or barrier semaphores. Data moves between devices by JAX's collectives and lax.ppermute only.
A program may use at most 64 MiB of HBM per device.

v0:
```python
import jax
import jax.numpy as jnp
from jax import lax
from jax.sharding import PartitionSpec as P

ITERS = 8
step_primal = 0.5
step_dual = 0.5


def per_device(
    blocks, block_cols, objective, lower_bound, upper_bound, right_side, primal_init, dual_init
):
    row_blocks = blocks.shape[0]
    slots = blocks.shape[1]
    width = blocks.shape[2]
    row_devices = lax.axis_size("row")
    col_devices = lax.axis_size("col")
    primal_len = objective.shape[0]
    dual_len = right_side.shape[0]
    col_blocks = primal_len * row_devices // width
    primal_total = float(primal_len * row_devices * col_devices)
    dual_total = float(dual_len * row_devices * col_devices)
    flat_cols = block_cols.reshape(-1)
    chosen = flat_cols[:, None] == jnp.arange(col_blocks, dtype=jnp.int32)[None, :]
    chosen_half = chosen.astype(jnp.bfloat16)
    chosen_full = chosen.astype(jnp.float32)
    history = []
    primal_slab, objective_slab, lower_slab, upper_slab = (
        lax.all_gather(primal_init, "row", axis=0, tiled=True),
        lax.all_gather(objective, "row", axis=0, tiled=True),
        lax.all_gather(lower_bound, "row", axis=0, tiled=True),
        lax.all_gather(upper_bound, "row", axis=0, tiled=True),
    )
    dual_slab, right_slab = (
        lax.all_gather(dual_init, "col", axis=0, tiled=True),
        lax.all_gather(right_side, "col", axis=0, tiled=True),
    )
    primal_offset = lax.axis_index("row") * primal_len
    dual_offset = lax.axis_index("col") * dual_len
    for iteration in range(ITERS):
        dual_half = dual_slab.astype(jnp.bfloat16)
        dual_amount = dual_half.shape[0] // width
        products = jnp.einsum(
            "rsab,ra->rsb",
            blocks,
            dual_half.reshape(dual_amount, width),
            preferred_element_type=jnp.float32,
        ).reshape(dual_amount * slots, width)
        gradient = lax.psum(
            jnp.dot(
                chosen_full.T,
                products,
                precision=lax.Precision.HIGHEST,
                preferred_element_type=jnp.float32,
            ).reshape(-1),
            "row",
        )
        primal_next = jnp.minimum(
            upper_slab,
            jnp.maximum(lower_slab, primal_slab - step_primal * (objective_slab - gradient)),
        )
        extrapolated = (2.0 * primal_next - primal_slab).astype(jnp.bfloat16)
        pick_amount = extrapolated.shape[0] // width
        picked = jnp.dot(
            chosen_half,
            extrapolated.reshape(pick_amount, width),
            preferred_element_type=jnp.float32,
        )
        shaped = picked.astype(jnp.bfloat16).reshape(row_blocks, slots, width)
        image_dual = lax.psum(
            jnp.einsum("rsab,rsb->ra", blocks, shaped, preferred_element_type=jnp.float32).reshape(
                -1
            ),
            "col",
        )
        dual_next = jnp.maximum(dual_slab + step_dual * (right_slab - image_dual), 0.0)
        primal_step = lax.dynamic_slice_in_dim(
            primal_next - primal_slab, primal_offset, primal_len, 0
        )
        dual_step = lax.dynamic_slice_in_dim(dual_next - dual_slab, dual_offset, dual_len, 0)
        summed = lax.psum(
            (jnp.sum(primal_step * primal_step), jnp.sum(dual_step * dual_step)), ("row", "col")
        )
        history.append(jnp.stack(summed))
        primal_slab = primal_next
        dual_slab = dual_next
    primal_out = lax.dynamic_slice_in_dim(primal_slab, primal_offset, primal_len, 0)
    dual_out = lax.dynamic_slice_in_dim(dual_slab, dual_offset, dual_len, 0)
    stacked = jnp.stack(history)
    totals = jnp.array([primal_total, dual_total], jnp.float32)
    step_norms = jnp.sqrt(stacked / totals[None, :])
    return (primal_out, dual_out, step_norms)


def solution(mesh):
    in_specs = (
        P("row", "col", None, None),
        P("row", "col"),
        P(("col", "row")),
        P(("col", "row")),
        P(("col", "row")),
        P(("row", "col")),
        P(("col", "row")),
        P(("row", "col")),
    )
    out_specs = (P(("col", "row")), P(("row", "col")), P())
    return jax.shard_map(
        per_device, mesh=mesh, in_specs=in_specs, out_specs=out_specs, check_vma=False
    )
```

profile of v0, /device:TPU:12, one launch (start us, length us, event | category | flops | bytes accessed | tf_op | source)
XLA Modules:
  0.0 513.0 jit_solution(17273579642622578398)
XLA Ops:
  0.7 0.8 copy.16
  1.5 8.2 %all_gather.22 = f32[4096]{0:T(1024)S(1)} all-gather(f32[1024]{0:T(1024)} %param.16), channel_id=1, replica_groups=mesh['row'=8,'col'=4] {'col'}, dimensions={0}, use_global_device_ids=true | all-gather | bytes 20480 | tf_op jit(solution)/shard_map/all_gather | solution.py:36
  9.7 2.8 fusion.27
  12.6 0.3 convolution_bitcast_fusion.7
  13.0 23.7 %psum.224 = f32[12288]{0:T(1024)S(1)} all-reduce(f32[12288]{0:T(1024)S(1)} %bitcast.198), channel_id=1, replica_groups=mesh['row'=8,'col'=4] {'row'}, use_global_device_ids=true, to_apply=%region_0.0 | all-reduce | flops 12288 | bytes 98304 | tf_op jit(solution)/shard_map/psum | solution.py:50
  36.6 14.3 %all-gather = f32[8,1,1536]{2,1,0:T(1,128)S(1)} all-gather(f32[1,1,1536]{2,1,0:T(1,128)S(1)} %reshape.200), channel_id=1, replica_groups=mesh['row'=8,'col'=4] {'row'}, dimensions={0}, use_global_device_ids=true | all-gather | bytes 55296 | tf_op jit(solution)/shard_map/all_gather | solution.py:33
  51.0 14.3 %all-gather.1 = f32[8,1,1536]{2,1,0:T(1,128)S(1)} all-gather(f32[1,1,1536]{2,1,0:T(1,128)S(1)} %reshape.202), channel_id=1, replica_groups=mesh['row'=8,'col'=4] {'row'}, dimensions={0}, use_global_device_ids=true | all-gather | bytes 55296 | tf_op jit(solution)/shard_map/all_gather | solution.py:32
  65.3 14.0 %all-gather.3 = f32[8,1,1536]{2,1,0:T(1,128)S(1)} all-gather(f32[1,1,1536]{2,1,0:T(1,128)S(1)} %reshape.206), channel_id=1, replica_groups=mesh['row'=8,'col'=4] {'row'}, dimensions={0}, use_global_device_ids=true | all-gather | bytes 55296 | tf_op jit(solution)/shard_map/all_gather | solution.py:31
  79.4 14.0 %all-gather.2 = f32[8,1,1536]{2,1,0:T(1,128)S(1)} all-gather(f32[1,1,1536]{2,1,0:T(1,128)S(1)} %reshape.204), channel_id=1, replica_groups=mesh['row'=8,'col'=4] {'row'}, dimensions={0}, use_global_device_ids=true | all-gather | bytes 55296 | tf_op jit(solution)/shard_map/all_gather | solution.py:30
  93.7 3.4 fusion.28
  97.1 15.1 %psum.225 = f32[4096]{0:T(1024)S(1)} all-reduce(f32[4096]{0:T(1024)S(1)} %bitcast.215), channel_id=1, replica_groups=mesh['row'=8,'col'=4] {'col'}, use_global_device_ids=true, to_apply=%region_1.0 | all-reduce | flops 4096 | bytes 32768 | tf_op jit(solution)/shard_map/psum | solution.py:71
  112.2 7.2 %all_gather.23 = f32[4096]{0:T(1024)S(1)} all-gather(f32[1024]{0:T(1024)S(1)} %copy-done.4), channel_id=1, replica_groups=mesh['row'=8,'col'=4] {'col'}, dimensions={0}, use_global_device_ids=true | all-gather | bytes 20480 | tf_op jit(solution)/shard_map/all_gather | solution.py:37
  119.4 2.8 fusion.29
  122.6 25.7 %psum.226 = f32[12288]{0:T(1024)S(1)} all-reduce(f32[12288]{0:T(1024)S(1)} %bitcast.199), channel_id=1, replica_groups=mesh['row'=8,'col'=4] {'row'}, use_global_device_ids=true, to_apply=%region_2.0 | all-reduce | flops 12288 | bytes 98304 | tf_op jit(solution)/shard_map/psum | solution.py:50
  148.6 3.4 fusion.30
  152.0 15.1 %psum.227 = f32[4096]{0:T(1024)S(1)} all-reduce(f32[4096]{0:T(1024)S(1)} %bitcast.217), channel_id=1, replica_groups=mesh['row'=8,'col'=4] {'col'}, use_global_device_ids=true, to_apply=%region_3.0 | all-reduce | flops 4096 | bytes 32768 | tf_op jit(solution)/shard_map/psum | solution.py:71
  167.1 2.8 fusion.31
  170.3 26.4 %psum.228 = f32[12288]{0:T(1024)S(1)} all-reduce(f32[12288]{0:T(1024)S(1)} %bitcast.200), channel_id=1, replica_groups=mesh['row'=8,'col'=4] {'row'}, use_global_device_ids=true, to_apply=%region_4.0 | all-reduce | flops 12288 | bytes 98304 | tf_op jit(solution)/shard_map/psum | solution.py:50
  196.9 3.4 fusion.32
  200.3 14.1 %psum.229 = f32[4096]{0:T(1024)S(1)} all-reduce(f32[4096]{0:T(1024)S(1)} %bitcast.219), channel_id=1, replica_groups=mesh['row'=8,'col'=4] {'col'}, use_global_device_ids=true, to_apply=%region_5.0 | all-reduce | flops 4096 | bytes 32768 | tf_op jit(solution)/shard_map/psum | solution.py:71
  214.4 2.8 fusion.33
  217.7 26.4 %psum.230 = f32[12288]{0:T(1024)S(1)} all-reduce(f32[12288]{0:T(1024)S(1)} %bitcast.201), channel_id=1, replica_groups=mesh['row'=8,'col'=4] {'row'}, use_global_device_ids=true, to_apply=%region_6.0 | all-reduce | flops 12288 | bytes 98304 | tf_op jit(solution)/shard_map/psum | solution.py:50
  244.3 3.4 fusion.34
  247.7 15.1 %psum.231 = f32[4096]{0:T(1024)S(1)} all-reduce(f32[4096]{0:T(1024)S(1)} %bitcast.221), channel_id=1, replica_groups=mesh['row'=8,'col'=4] {'col'}, use_global_device_ids=true, to_apply=%region_7.0 | all-reduce | flops 4096 | bytes 32768 | tf_op jit(solution)/shard_map/psum | solution.py:71
  262.7 2.8 fusion.35
  266.0 26.4 %psum.232 = f32[12288]{0:T(1024)S(1)} all-reduce(f32[12288]{0:T(1024)S(1)} %bitcast.202), channel_id=1, replica_groups=mesh['row'=8,'col'=4] {'row'}, use_global_device_ids=true, to_apply=%region_8.0 | all-reduce | flops 12288 | bytes 98304 | tf_op jit(solution)/shard_map/psum | solution.py:50
  292.6 3.4 fusion.36
  296.0 14.1 %psum.233 = f32[4096]{0:T(1024)S(1)} all-reduce(f32[4096]{0:T(1024)S(1)} %bitcast.223), channel_id=1, replica_groups=mesh['row'=8,'col'=4] {'col'}, use_global_device_ids=true, to_apply=%region_9.0 | all-reduce | flops 4096 | bytes 32768 | tf_op jit(solution)/shard_map/psum | solution.py:71
  310.1 2.8 fusion.37
  313.3 26.4 %psum.234 = f32[12288]{0:T(1024)S(1)} all-reduce(f32[12288]{0:T(1024)S(1)} %bitcast.203), channel_id=1, replica_groups=mesh['row'=8,'col'=4] {'row'}, use_global_device_ids=true, to_apply=%region_10.0 | all-reduce | flops 12288 | bytes 98304 | tf_op jit(solution)/shard_map/psum | solution.py:50
  340.0 3.4 fusion.38
  343.4 15.0 %psum.235 = f32[4096]{0:T(1024)S(1)} all-reduce(f32[4096]{0:T(1024)S(1)} %bitcast.225), channel_id=1, replica_groups=mesh['row'=8,'col'=4] {'col'}, use_global_device_ids=true, to_apply=%region_11.0 | all-reduce | flops 4096 | bytes 32768 | tf_op jit(solution)/shard_map/psum | solution.py:71
  358.4 2.8 fusion.39
  361.6 26.4 %psum.236 = f32[12288]{0:T(1024)S(1)} all-reduce(f32[12288]{0:T(1024)S(1)} %bitcast.204), channel_id=1, replica_groups=mesh['row'=8,'col'=4] {'row'}, use_global_device_ids=true, to_apply=%region_12.0 | all-reduce | flops 12288 | bytes 98304 | tf_op jit(solution)/shard_map/psum | solution.py:50
  388.3 3.4 fusion.40
  391.7 14.1 %psum.237 = f32[4096]{0:T(1024)S(1)} all-reduce(f32[4096]{0:T(1024)S(1)} %bitcast.227), channel_id=1, replica_groups=mesh['row'=8,'col'=4] {'col'}, use_global_device_ids=true, to_apply=%region_13.0 | all-reduce | flops 4096 | bytes 32768 | tf_op jit(solution)/shard_map/psum | solution.py:71
  405.8 2.8 fusion.41
  409.0 26.4 %psum.238 = f32[12288]{0:T(1024)S(1)} all-reduce(f32[12288]{0:T(1024)S(1)} %bitcast.205), channel_id=1, replica_groups=mesh['row'=8,'col'=4] {'row'}, use_global_device_ids=true, to_apply=%region_14.0 | all-reduce | flops 12288 | bytes 98304 | tf_op jit(solution)/shard_map/psum | solution.py:50
  435.6 3.4 fusion.42
  439.1 15.0 %psum.239 = f32[4096]{0:T(1024)S(1)} all-reduce(f32[4096]{0:T(1024)S(1)} %bitcast.229), channel_id=1, replica_groups=mesh['row'=8,'col'=4] {'col'}, use_global_device_ids=true, to_apply=%region_15.0 | all-reduce | flops 4096 | bytes 32768 | tf_op jit(solution)/shard_map/psum | solution.py:71
  454.1 1.3 multiply_reduce_fusion.7
  455.4 1.4 multiply_reduce_fusion
  456.7 44.3 %all-reduce = (f32[1]{0:T(128)}, f32[1]{0:T(128)}, f32[1]{0:T(128)}, f32[1]{0:T(128)}, f32[1]{0:T(128)}, /*index=5*/f32[1]{0:T(128)}, f32[1]{0:T(128)}, f32[1]{0...) all-reduce(f32[1]{0:T(128)} %bitcast.21, ...), channel_id=1, replica_groups=mesh['row'=8,'col'=4] {'row','col'}, use_global_device_ids=true, to_apply=%region_19.0 | all-reduce | flops 16 | bytes 128 | tf_op jit(solution)/shard_map/psum | solution.py:82
  501.1 2.6 maximum_bitcast_fusion.6
  503.9 2.6 maximum_bitcast_fusion.4
  506.7 2.6 maximum_bitcast_fusion.2
  509.6 2.5 maximum_bitcast_fusion
  512.3 0.6 multiply_sqrt_fusion
  (122 shorter events, 5.9 us)
Async XLA Ops:
  0.6 36.0 %copy-start = (f32[1536]{0:T(1024)S(1)}, f32[1536]{0:T(1024)}, u32[]{:S(2)}) copy-start(f32[1536]{0:T(1024)} %param.13) | copy-start | bytes 18436
  0.6 50.3 %copy-start.1 = (f32[1536]{0:T(1024)S(1)}, f32[1536]{0:T(1024)}, u32[]{:S(2)}) copy-start(f32[1536]{0:T(1024)} %param.12) | copy-start | bytes 18436
  0.7 64.7 %copy-start.2 = (f32[1536]{0:T(1024)S(1)}, f32[1536]{0:T(1024)}, u32[]{:S(2)}) copy-start(f32[1536]{0:T(1024)} %param.11) | copy-start | bytes 18436
  0.7 78.7 %copy-start.3 = (f32[1536]{0:T(1024)S(1)}, f32[1536]{0:T(1024)}, u32[]{:S(2)}) copy-start(f32[1536]{0:T(1024)} %param.15) | copy-start | bytes 18436
  9.7 102.4 %copy-start.4 = (f32[1024]{0:T(1024)S(1)}, f32[1024]{0:T(1024)}, u32[]{:S(2)}) copy-start(f32[1024]{0:T(1024)} %param.14) | copy-start | bytes 12292
  405.8 106.5 %copy-start.5 = (f32[2]{0:T(128)S(1)}, f32[2]{0:T(128)}, u32[]{:S(2)}) copy-start(f32[2]{0:T(128)} %constant.32) | copy-start | bytes 28
where the time goes:
time: 514 us; the launch traced here: 513 us
  blocking collectives  442 us (86%)
  matrix products  53.4 us (10%)
  other arithmetic  14 us (3%)
    psum x8, blocking collectives, per_device(): lax.psum(jnp.dot(chosen_full.T, products, precision=lax.Precision.HIGHEST...  208 us
    psum x8, blocking collectives, per_device(): lax.psum(jnp.einsum('rsab,rsb->ra', blocks, shaped, preferred_element_typ...  118 us
    psum x1, blocking collectives, per_device(): lax.psum((jnp.sum(primal_step * primal_step), jnp.sum(dual_step * dual_st...  44.3 us
    dot_general x8, matrix products, per_device(): jnp.einsum('rsab,rsb->ra', blocks, shaped, preferred_element_type=jnp.flo...  26.9 us
    dot_general x8, matrix products, per_device(): jnp.einsum('rsab,ra->rsb', blocks, dual_half.reshape(dual_amount, width),...  22.7 us
    all_gather x1, blocking collectives, per_device(): lax.all_gather(lower_bound, 'row', axis=0, tiled=True)  14.3 us
    all_gather x1, blocking collectives, per_device(): lax.all_gather(upper_bound, 'row', axis=0, tiled=True)  14.3 us
    all_gather x1, blocking collectives, per_device(): lax.all_gather(primal_init, 'row', axis=0, tiled=True)  14 us

commit v1 on v0

--- a/solution.py
+++ b/solution.py
@@ -47,14 +47,17 @@
             dual_half.reshape(dual_amount, width),
             preferred_element_type=jnp.float32,
         ).reshape(dual_amount * slots, width)
-        gradient = lax.psum(
-            jnp.dot(
-                chosen_full.T,
-                products,
-                precision=lax.Precision.HIGHEST,
-                preferred_element_type=jnp.float32,
-            ).reshape(-1),
-            "row",
+        gradient = jnp.sum(
+            lax.all_gather(
+                jnp.dot(
+                    chosen_full.T,
+                    products,
+                    precision=lax.Precision.HIGHEST,
+                    preferred_element_type=jnp.float32,
+                ).reshape(-1),
+                "row",
+            ),
+            axis=0,
         )
         primal_next = jnp.minimum(
             upper_slab,

time: 514 us -> 423 us (0.82)
  blocking collectives: 442 us -> 347 us
    psum x8 -> x0, blocking collectives: 208 us -> none  [per_device(): lax.psum(jnp.dot(chosen_full.T, products, precision=lax.Precision.HIGHEST...]
    all_gather x0 -> x8, blocking collectives: none -> 116 us  [per_device(): lax.all_gather(jnp.dot(chosen_full.T, products, precision=lax.Precision.H...]
where the time goes in v1:
time: 423 us; the launch traced here: 421 us
  blocking collectives  347 us (82%)
  matrix products  53.4 us (13%)
  other arithmetic  16.3 us (4%)
    psum x8, blocking collectives, per_device(): lax.psum(jnp.einsum('rsab,rsb->ra', blocks, shaped, preferred_element_typ...  118 us
    all_gather x8, blocking collectives, per_device(): lax.all_gather(jnp.dot(chosen_full.T, products, precision=lax.Precision.H...  116 us
    psum x1, blocking collectives, per_device(): lax.psum((jnp.sum(primal_step * primal_step), jnp.sum(dual_step * dual_st...  41.8 us
    dot_general x8, matrix products, per_device(): jnp.einsum('rsab,rsb->ra', blocks, shaped, preferred_element_type=jnp.flo...  26.9 us
    dot_general x8, matrix products, per_device(): jnp.einsum('rsab,ra->rsb', blocks, dual_half.reshape(dual_amount, width),...  22.7 us
    all_gather x1, blocking collectives, per_device(): lax.all_gather(upper_bound, 'row', axis=0, tiled=True)  14.1 us
    all_gather x1, blocking collectives, per_device(): lax.all_gather(lower_bound, 'row', axis=0, tiled=True)  14 us
    all_gather x1, blocking collectives, per_device(): lax.all_gather(objective, 'row', axis=0, tiled=True)  14 us

profile of v1, /device:TPU:12, one launch (start us, length us, event | category | flops | bytes accessed | tf_op | source)
XLA Modules:
  0.0 421.3 jit_solution(6010542728809269811)
XLA Ops:
  0.7 0.8 copy.16
  1.5 8.2 %all_gather.46 = f32[4096]{0:T(1024)S(1)} all-gather(f32[1024]{0:T(1024)} %param.16), channel_id=1, replica_groups=mesh['row'=8,'col'=4] {'col'}, dimensions={0}, use_global_device_ids=true | all-gather | bytes 20480 | tf_op jit(solution)/shard_map/all_gather | solution.py:36
  9.7 2.8 fusion.35
  13.0 14.8 %all-gather.4 = f32[8,1,12288]{2,1,0:T(1,128)S(1)} all-gather(f32[1,1,12288]{2,1,0:T(1,128)S(1)} %reshape.176), channel_id=1, replica_groups=mesh['row'=8,'col'=4] {'row'}, dimensions={0}, use_global_device_ids=true | all-gather | bytes 442368 | tf_op jit(solution)/shard_map/all_gather | solution.py:51
  27.7 0.3 reduce_sum.216
  28.0 14.1 %all-gather = f32[8,1,1536]{2,1,0:T(1,128)S(1)} all-gather(f32[1,1,1536]{2,1,0:T(1,128)S(1)} %reshape.168), channel_id=1, replica_groups=mesh['row'=8,'col'=4] {'row'}, dimensions={0}, use_global_device_ids=true | all-gather | bytes 55296 | tf_op jit(solution)/shard_map/all_gather | solution.py:33
  42.1 14.0 %all-gather.1 = f32[8,1,1536]{2,1,0:T(1,128)S(1)} all-gather(f32[1,1,1536]{2,1,0:T(1,128)S(1)} %reshape.170), channel_id=1, replica_groups=mesh['row'=8,'col'=4] {'row'}, dimensions={0}, use_global_device_ids=true | all-gather | bytes 55296 | tf_op jit(solution)/shard_map/all_gather | solution.py:32
  56.2 14.0 %all-gather.3 = f32[8,1,1536]{2,1,0:T(1,128)S(1)} all-gather(f32[1,1,1536]{2,1,0:T(1,128)S(1)} %reshape.174), channel_id=1, replica_groups=mesh['row'=8,'col'=4] {'row'}, dimensions={0}, use_global_device_ids=true | all-gather | bytes 55296 | tf_op jit(solution)/shard_map/all_gather | solution.py:31
  70.2 14.0 %all-gather.2 = f32[8,1,1536]{2,1,0:T(1,128)S(1)} all-gather(f32[1,1,1536]{2,1,0:T(1,128)S(1)} %reshape.172), channel_id=1, replica_groups=mesh['row'=8,'col'=4] {'row'}, dimensions={0}, use_global_device_ids=true | all-gather | bytes 55296 | tf_op jit(solution)/shard_map/all_gather | solution.py:30
  84.5 3.4 fusion.36
  87.9 15.1 %psum.168 = f32[4096]{0:T(1024)S(1)} all-reduce(f32[4096]{0:T(1024)S(1)} %bitcast.183), channel_id=1, replica_groups=mesh['row'=8,'col'=4] {'col'}, use_global_device_ids=true, to_apply=%region_1.0 | all-reduce | flops 4096 | bytes 32768 | tf_op jit(solution)/shard_map/psum | solution.py:74
  103.0 7.2 %all_gather.48 = f32[4096]{0:T(1024)S(1)} all-gather(f32[1024]{0:T(1024)S(1)} %copy-done.4), channel_id=1, replica_groups=mesh['row'=8,'col'=4] {'col'}, dimensions={0}, use_global_device_ids=true | all-gather | bytes 20480 | tf_op jit(solution)/shard_map/all_gather | solution.py:37
  110.2 2.8 fusion.37
  113.5 14.5 %all-gather.5 = f32[8,1,12288]{2,1,0:T(1,128)S(1)} all-gather(f32[1,1,12288]{2,1,0:T(1,128)S(1)} %reshape.178), channel_id=1, replica_groups=mesh['row'=8,'col'=4] {'row'}, dimensions={0}, use_global_device_ids=true | all-gather | bytes 442368 | tf_op jit(solution)/shard_map/all_gather | solution.py:51
  128.5 3.4 fusion.38
  131.9 15.1 %psum.169 = f32[4096]{0:T(1024)S(1)} all-reduce(f32[4096]{0:T(1024)S(1)} %bitcast.185), channel_id=1, replica_groups=mesh['row'=8,'col'=4] {'col'}, use_global_device_ids=true, to_apply=%region_3.0 | all-reduce | flops 4096 | bytes 32768 | tf_op jit(solution)/shard_map/psum | solution.py:74
  147.0 2.8 fusion.39
  150.2 14.5 %all-gather.6 = f32[8,1,12288]{2,1,0:T(1,128)S(1)} all-gather(f32[1,1,12288]{2,1,0:T(1,128)S(1)} %reshape.180), channel_id=1, replica_groups=mesh['row'=8,'col'=4] {'row'}, dimensions={0}, use_global_device_ids=true | all-gather | bytes 442368 | tf_op jit(solution)/shard_map/all_gather | solution.py:51
  165.3 3.4 fusion.40
  168.7 14.1 %psum.170 = f32[4096]{0:T(1024)S(1)} all-reduce(f32[4096]{0:T(1024)S(1)} %bitcast.187), channel_id=1, replica_groups=mesh['row'=8,'col'=4] {'col'}, use_global_device_ids=true, to_apply=%region_5.0 | all-reduce | flops 4096 | bytes 32768 | tf_op jit(solution)/shard_map/psum | solution.py:74
  182.9 2.8 fusion.41
  186.1 14.7 %all-gather.7 = f32[8,1,12288]{2,1,0:T(1,128)S(1)} all-gather(f32[1,1,12288]{2,1,0:T(1,128)S(1)} %reshape.182), channel_id=1, replica_groups=mesh['row'=8,'col'=4] {'row'}, dimensions={0}, use_global_device_ids=true | all-gather | bytes 442368 | tf_op jit(solution)/shard_map/all_gather | solution.py:51
  201.4 3.4 fusion.42
  204.8 15.1 %psum.171 = f32[4096]{0:T(1024)S(1)} all-reduce(f32[4096]{0:T(1024)S(1)} %bitcast.189), channel_id=1, replica_groups=mesh['row'=8,'col'=4] {'col'}, use_global_device_ids=true, to_apply=%region_7.0 | all-reduce | flops 4096 | bytes 32768 | tf_op jit(solution)/shard_map/psum | solution.py:74
  219.8 2.8 fusion.43
  223.1 14.5 %all-gather.8 = f32[8,1,12288]{2,1,0:T(1,128)S(1)} all-gather(f32[1,1,12288]{2,1,0:T(1,128)S(1)} %reshape.184), channel_id=1, replica_groups=mesh['row'=8,'col'=4] {'row'}, dimensions={0}, use_global_device_ids=true | all-gather | bytes 442368 | tf_op jit(solution)/shard_map/all_gather | solution.py:51
  238.1 3.4 fusion.44
  241.5 14.1 %psum.172 = f32[4096]{0:T(1024)S(1)} all-reduce(f32[4096]{0:T(1024)S(1)} %bitcast.191), channel_id=1, replica_groups=mesh['row'=8,'col'=4] {'col'}, use_global_device_ids=true, to_apply=%region_9.0 | all-reduce | flops 4096 | bytes 32768 | tf_op jit(solution)/shard_map/psum | solution.py:74
  255.6 2.8 fusion.45
  258.9 14.5 %all-gather.9 = f32[8,1,12288]{2,1,0:T(1,128)S(1)} all-gather(f32[1,1,12288]{2,1,0:T(1,128)S(1)} %reshape.186), channel_id=1, replica_groups=mesh['row'=8,'col'=4] {'row'}, dimensions={0}, use_global_device_ids=true | all-gather | bytes 442368 | tf_op jit(solution)/shard_map/all_gather | solution.py:51
  273.9 3.4 fusion.46
  277.3 15.1 %psum.173 = f32[4096]{0:T(1024)S(1)} all-reduce(f32[4096]{0:T(1024)S(1)} %bitcast.193), channel_id=1, replica_groups=mesh['row'=8,'col'=4] {'col'}, use_global_device_ids=true, to_apply=%region_11.0 | all-reduce | flops 4096 | bytes 32768 | tf_op jit(solution)/shard_map/psum | solution.py:74
  292.4 2.8 fusion.47
  295.6 14.5 %all-gather.10 = f32[8,1,12288]{2,1,0:T(1,128)S(1)} all-gather(f32[1,1,12288]{2,1,0:T(1,128)S(1)} %reshape.188), channel_id=1, replica_groups=mesh['row'=8,'col'=4] {'row'}, dimensions={0}, use_global_device_ids=true | all-gather | bytes 442368 | tf_op jit(solution)/shard_map/all_gather | solution.py:51
  310.6 3.4 fusion.48
  314.0 14.1 %psum.174 = f32[4096]{0:T(1024)S(1)} all-reduce(f32[4096]{0:T(1024)S(1)} %bitcast.195), channel_id=1, replica_groups=mesh['row'=8,'col'=4] {'col'}, use_global_device_ids=true, to_apply=%region_13.0 | all-reduce | flops 4096 | bytes 32768 | tf_op jit(solution)/shard_map/psum | solution.py:74
  328.2 2.8 fusion.49
  331.4 14.5 %all-gather.11 = f32[8,1,12288]{2,1,0:T(1,128)S(1)} all-gather(f32[1,1,12288]{2,1,0:T(1,128)S(1)} %reshape.190), channel_id=1, replica_groups=mesh['row'=8,'col'=4] {'row'}, dimensions={0}, use_global_device_ids=true | all-gather | bytes 442368 | tf_op jit(solution)/shard_map/all_gather | solution.py:51
  346.4 3.4 fusion.50
  349.8 15.1 %psum.175 = f32[4096]{0:T(1024)S(1)} all-reduce(f32[4096]{0:T(1024)S(1)} %bitcast.197), channel_id=1, replica_groups=mesh['row'=8,'col'=4] {'col'}, use_global_device_ids=true, to_apply=%region_15.0 | all-reduce | flops 4096 | bytes 32768 | tf_op jit(solution)/shard_map/psum | solution.py:74
  364.9 1.3 multiply_reduce_fusion.7
  366.2 1.4 multiply_reduce_fusion
  367.6 41.8 %all-reduce = (f32[1]{0:T(128)}, f32[1]{0:T(128)}, f32[1]{0:T(128)}, f32[1]{0:T(128)}, f32[1]{0:T(128)}, /*index=5*/f32[1]{0:T(128)}, f32[1]{0:T(128)}, f32[1]{0...) all-reduce(f32[1]{0:T(128)} %bitcast.21, ...), channel_id=1, replica_groups=mesh['row'=8,'col'=4] {'row','col'}, use_global_device_ids=true, to_apply=%region_19.0 | all-reduce | flops 16 | bytes 128 | tf_op jit(solution)/shard_map/psum | solution.py:85
  409.4 2.6 maximum_bitcast_fusion.6
  412.2 2.6 maximum_bitcast_fusion.4
  415.0 2.6 maximum_bitcast_fusion.2
  417.9 2.5 maximum_bitcast_fusion
  420.7 0.6 multiply_sqrt_fusion
  (130 shorter events, 8.4 us)
Async XLA Ops:
  0.6 27.4 %copy-start = (f32[1536]{0:T(1024)S(1)}, f32[1536]{0:T(1024)}, u32[]{:S(2)}) copy-start(f32[1536]{0:T(1024)} %param.13) | copy-start | bytes 18436
  0.6 41.5 %copy-start.1 = (f32[1536]{0:T(1024)S(1)}, f32[1536]{0:T(1024)}, u32[]{:S(2)}) copy-start(f32[1536]{0:T(1024)} %param.12) | copy-start | bytes 18436
  0.7 55.5 %copy-start.2 = (f32[1536]{0:T(1024)S(1)}, f32[1536]{0:T(1024)}, u32[]{:S(2)}) copy-start(f32[1536]{0:T(1024)} %param.11) | copy-start | bytes 18436
  0.7 69.6 %copy-start.3 = (f32[1536]{0:T(1024)S(1)}, f32[1536]{0:T(1024)}, u32[]{:S(2)}) copy-start(f32[1536]{0:T(1024)} %param.15) | copy-start | bytes 18436
  12.5 90.4 %copy-start.4 = (f32[1024]{0:T(1024)S(1)}, f32[1024]{0:T(1024)}, u32[]{:S(2)}) copy-start(f32[1024]{0:T(1024)} %param.14) | copy-start | bytes 12292
  331.0 89.7 %copy-start.5 = (f32[2]{0:T(128)S(1)}, f32[2]{0:T(128)}, u32[]{:S(2)}) copy-start(f32[2]{0:T(128)} %constant.32) | copy-start | bytes 28
